TPU v7x, 512 devices: a whole 4x4x16 slice. The times are simulated.
512 devices in a mesh: dp: 128 (over x, y, z_hi, core), rep: 4 (over z_lo).
Axes of the slice: x: 4, y: 4, z: 16 (z_hi: 4, z_lo: 4; z = z_hi * 4 + z_lo), core: 2. Of those that a mesh axis runs over, the one named last changes fastest.
Arguments:
- student_in: bfloat16 [262144, 320], P(('dp', 'rep')), may hold values from -6 to 6
- target_in: bfloat16 [262144, 320], P(('dp', 'rep')), may hold values from -6 to 6
- timesteps: int32 [1024], P(('dp', 'rep')), may hold values from 20 to 999
- student_win: float32 [1280, 320], P('dp'), may hold values from -0.3125 to 0.3125
- student_wout: float32 [640, 320], P('dp'), may hold values from -0.25 to 0.25
- student_wtime: float32 [640, 320], P('dp'), may hold values from -0.25 to 0.25
- student_gain: float32 [320], replicated, may hold values from 0.5 to 1.5
- student_bias: float32 [320], replicated, may hold values from -3 to 3
- target_win: float32 [1280, 320], P('dp'), may hold values from -0.3125 to 0.3125
- target_wout: float32 [640, 320], P('dp'), may hold values from -0.25 to 0.25
- target_wtime: float32 [640, 320], P('dp'), may hold values from -0.25 to 0.25
- target_gain: float32 [320], replicated, may hold values from 0.5 to 1.5
- target_bias: float32 [320], replicated, may hold values from -3 to 3
Outputs:
- grad_win: float32 [1280, 320], P('dp')
- grad_wout: float32 [640, 320], P('dp')
- grad_wtime: float32 [640, 320], P('dp')
- grad_gain: float32 [320], replicated
- grad_bias: float32 [320], replicated
- ema_win: float32 [1280, 320], P('dp')
- ema_wout: float32 [640, 320], P('dp')
- ema_wtime: float32 [640, 320], P('dp')
- ema_gain: float32 [320], replicated
- ema_bias: float32 [320], replicated
Inputs may be any that keep to these rules, and one draw needn't show every extreme that they name: `timesteps`: student timestep of each sample; the target is evaluated at 20 steps earlier.
All inputs are finite; a program needn't handle non-finite values.
Results may differ from a plain program's by a relative error of at most 0.004.
The roundings to bfloat16 on the way count: a program that leaves them out, or rounds other values in their place, can miss the bound.
Values may be sent and summed in bfloat16 or wider, within the bound.
A program may use at most 64 MiB of HBM per device.

v0:
```python
import functools
import math

import jax
import jax.numpy as jnp
from jax import lax
from jax.sharding import Mesh
from jax.sharding import PartitionSpec as P

SKIP = 20
DP = ("dp_0", "dp_1", "dp_2", "dp_3")
DP_REP = ("dp_0", "dp_1", "dp_2", "dp_3", "rep")


ema_decay = 0.95
learn_rate = 0.05


def copy_for_each(shard, axis):
    peers = lax.axis_size(axis)
    return lax.all_to_all(
        jnp.broadcast_to(shard[None], (peers, *shard.shape)), axis, 0, 0, tiled=True
    )


def laid_out(tiles, dim):
    lengths = list(tiles.shape[1:])
    lengths[dim] *= tiles.shape[0]
    return jnp.moveaxis(tiles, 0, dim).reshape(lengths)


def gathered_by_axis(shard, axes, dim):
    far, near = axes
    initial = copy_for_each(shard, far)
    tiles = jnp.swapaxes(copy_for_each(initial, near), 0, 1)
    return laid_out(tiles.reshape(-1, *shard.shape), dim)


def in_one_piece(arrays, axis, dim, along):
    both = jnp.concatenate(arrays, axis=along)
    whole, at, gathered = (gathered_by_axis(both, axis, dim), 0, [])
    for a in arrays:
        gathered.append(lax.slice_in_dim(whole, at, at + a.shape[along], axis=along))
        at += a.shape[along]
    return tuple(gathered)


def cut_along(shard, dim, peers):
    before, after = (shard.shape[:dim], shard.shape[dim + 1 :])
    return jnp.moveaxis(shard.reshape(*before, peers, -1, *after), dim, 0)


def sum_at_owner(shard, axis, dim):
    peers = lax.axis_size(axis)
    tiles = lax.all_to_all(cut_along(shard, dim, peers), axis, 0, 0, tiled=True)
    return jnp.sum(tiles.astype(jnp.float32), axis=0)


def side_by_side(arrays, axis, dim, along):
    ends, at = ([], 0)
    for a in arrays[:-1]:
        at += a.shape[along]
        ends.append(at)
    both = jnp.concatenate(arrays, axis=along)
    return tuple(jnp.split(sum_at_owner(both, axis, dim), ends, axis=along))


def sum_at_owner_2(shard, axis, dim):
    tiles = cut_along(shard, dim, lax.axis_size(axis))
    arrived = lax.all_to_all(tiles, axis, split_axis=0, concat_axis=0, tiled=True)
    return arrived.sum(axis=0)


def sum_by_axis(shard, axes, dim):
    far, near = axes
    own = sum_at_owner_2(cut_along(shard, dim, lax.axis_size(far)), near, dim + 1)
    return jnp.sum(lax.all_to_all(own, far, 0, 0, tiled=True), axis=0)


def side_by_side_2(arrays, axis, dim, along):
    both = jnp.concatenate(arrays, axis=along)
    whole, at, gathered = (sum_by_axis(both, axis, dim), 0, [])
    for a in arrays:
        gathered.append(lax.slice_in_dim(whole, at, at + a.shape[along], axis=along))
        at += a.shape[along]
    return tuple(gathered)


def rows_first(arrays, axis, dims):
    turned = [jnp.moveaxis(a, dim, 0) for a, dim in zip(arrays, dims)]
    widths = [t[0].size for t in turned]
    both = jnp.concatenate([t.reshape(-1, w) for t, w in zip(turned, widths)], axis=1)
    whole = lax.all_gather(both, axis, axis=0, tiled=True)
    tiles = jnp.split(whole, [sum(widths[:k]) for k in range(1, len(widths))], axis=1)
    return tuple(
        (
            jnp.moveaxis(b.reshape(-1, *t.shape[1:]), 0, dim)
            for b, t, dim in zip(tiles, turned, dims)
        )
    )


def by_axis(shard, axes):
    return functools.reduce(lax.psum, axes, shard)


def sinusoid(step_ids, width):
    half_width = width // 2
    frequency = jnp.exp(-math.log(10000.0) * jnp.arange(half_width, dtype=jnp.float32) / half_width)
    angles = step_ids.astype(jnp.float32)[:, None] * frequency[None, :]
    return jnp.concatenate([jnp.cos(angles), jnp.sin(angles)], axis=1)


def gelu_tanh(value):
    inner = 0.7978845608 * (value + 0.044715 * value * value * value)
    return 0.5 * value * (1.0 + jnp.tanh(inner))


def gelu_slope(value):
    tangent = jnp.tanh(0.7978845608 * (value + 0.044715 * value * value * value))
    return 0.5 * (1.0 + tangent) + 0.5 * value * (1.0 - tangent * tangent) * 0.7978845608 * (
        1.0 + 0.134145 * value * value
    )


def contract_last(left, right):
    return lax.dot_general(
        left, right, (((1,), (1,)), ((), ())), preferred_element_type=jnp.float32
    )


def contract_first(left, right):
    return lax.dot_general(
        left, right, (((0,), (0,)), ((), ())), preferred_element_type=jnp.float32
    )


def forward(tok_rows, step_ids, w_in, w_out, w_time, gain, bias):
    time_feat = jax.nn.silu(sinusoid(step_ids, w_time.shape[0])).astype(jnp.bfloat16)
    embedding = jnp.dot(time_feat, w_time, preferred_element_type=jnp.float32)
    samples = step_ids.shape[0]
    width = tok_rows.shape[1]
    summed = tok_rows.astype(jnp.float32).reshape(samples, -1, width) + embedding[:, None, :]
    summed = summed.reshape(-1, width)
    center = summed - jnp.mean(summed, axis=1, keepdims=True)
    inv_std = lax.rsqrt(jnp.mean(center * center, axis=1, keepdims=True) + 1e-05)
    normed = center * inv_std
    normed_b = (normed * gain + bias).astype(jnp.bfloat16)
    mixed = contract_last(normed_b, w_in)
    hidden_count = w_out.shape[0]
    gate_part = mixed[:, :hidden_count]
    up_part = mixed[:, hidden_count:]
    gelu_gate = gelu_tanh(gate_part)
    hidden = (gelu_gate * up_part).astype(jnp.bfloat16)
    output = summed + jnp.dot(hidden, w_out, preferred_element_type=jnp.float32)
    return (output, (time_feat, normed, inv_std, normed_b, gate_part, up_part, gelu_gate, hidden))


def backward(grad_y, saved, w_in, w_out, gain):
    time_feat, normed, inv_std, normed_b, gate_part, up_part, gelu_gate, hidden = saved
    grad_yb = grad_y.astype(jnp.bfloat16)
    grad_h = contract_last(grad_yb, w_out)
    grad_mix = jnp.concatenate(
        [grad_h * up_part * gelu_slope(gate_part), grad_h * gelu_gate], axis=1
    ).astype(jnp.bfloat16)
    grad_z = jnp.dot(grad_mix, w_in, preferred_element_type=jnp.float32)
    grad_gain = jnp.sum(grad_z * normed, axis=0)
    grad_bias = jnp.sum(grad_z, axis=0)
    grad_n = grad_z * gain
    grad_s = grad_y + inv_std * (
        grad_n
        - jnp.mean(grad_n, axis=1, keepdims=True)
        - normed * jnp.mean(grad_n * normed, axis=1, keepdims=True)
    )
    samples = time_feat.shape[0]
    grad_emb = jnp.sum(grad_s.reshape(samples, -1, grad_s.shape[1]), axis=1)
    grad_time = lax.dot_general(
        time_feat.astype(jnp.float32),
        grad_emb,
        (((0,), (0,)), ((), ())),
        precision=lax.Precision.HIGHEST,
        preferred_element_type=jnp.float32,
    )
    return (grad_yb, grad_mix, grad_gain, grad_bias, grad_time)


def fetch(piece_in, piece_out, piece_time):
    return (
        gathered_by_axis(piece_in, (("dp_0", "dp_1", "dp_2"), "dp_3"), 0),
        *in_one_piece((piece_out, piece_time), (("dp_0", "dp_1", "dp_2"), "dp_3"), 0, 1),
    )


def per_device(
    student_in,
    target_in,
    timesteps,
    student_win,
    student_wout,
    student_wtime,
    student_gain,
    student_bias,
    target_win,
    target_wout,
    target_wtime,
    target_gain,
    target_bias,
):
    s_in, s_out, s_time = fetch(
        student_win.astype(jnp.bfloat16),
        student_wout.astype(jnp.bfloat16),
        student_wtime.astype(jnp.bfloat16),
    )
    student_out, saved = forward(
        student_in, timesteps, s_in, s_out, s_time, student_gain, student_bias
    )
    t_in, t_out, t_time = fetch(
        target_win.astype(jnp.bfloat16),
        target_wout.astype(jnp.bfloat16),
        target_wtime.astype(jnp.bfloat16),
    )
    target_out, unused = forward(
        target_in, timesteps - SKIP, t_in, t_out, t_time, target_gain, target_bias
    )
    grad_y = (student_out - target_out) / student_in.shape[0]
    back_in, back_out = (s_in, s_out)
    grad_yb, grad_mix, grad_gain, grad_bias, grad_time = backward(
        grad_y, saved, back_in, back_out, student_gain
    )
    normed_b = saved[3]
    hidden = saved[7]
    full_in = contract_first(grad_mix, normed_b)
    full_out = contract_first(hidden, grad_yb)
    column_in, column_out, column_time = side_by_side(
        (
            full_in.astype(jnp.bfloat16),
            full_out.astype(jnp.bfloat16),
            grad_time.astype(jnp.bfloat16),
        ),
        "rep",
        1,
        0,
    )
    owner_in, owner_out, owner_time = (
        sum_by_axis(column_in, (("dp_0", "dp_1", "dp_2"), "dp_3"), 0),
        *side_by_side_2((column_out, column_time), (("dp_0", "dp_1", "dp_2"), "dp_3"), 0, 1),
    )
    shard_in, shard_out, shard_time = rows_first(
        (owner_in, owner_out, owner_time), "rep", (1, 1, 1)
    )
    total_gain, total_bias = (by_axis(grad_gain, DP_REP), by_axis(grad_bias, DP_REP))

    def average(target_p, student_p, grad_p):
        return ema_decay * target_p + (1.0 - ema_decay) * (student_p - learn_rate * grad_p)

    return (
        shard_in,
        shard_out,
        shard_time,
        total_gain,
        total_bias,
        average(target_win, student_win, shard_in),
        average(target_wout, student_wout, shard_out),
        average(target_wtime, student_wtime, shard_time),
        average(target_gain, student_gain, total_gain),
        average(target_bias, student_bias, total_bias),
    )


def solution(mesh):
    split = Mesh(
        mesh.devices.reshape(4, 4, 4, 2, mesh.shape["rep"]), ("dp_0", "dp_1", "dp_2", "dp_3", "rep")
    )
    return jax.shard_map(
        per_device,
        mesh=split,
        in_specs=(
            P(DP_REP, None),
            P(DP_REP, None),
            P(DP_REP),
            P(DP, None),
            P(DP, None),
            P(DP, None),
            P(),
            P(),
            P(DP, None),
            P(DP, None),
            P(DP, None),
            P(),
            P(),
        ),
        out_specs=(
            P(DP, None),
            P(DP, None),
            P(DP, None),
            P(),
            P(),
            P(DP, None),
            P(DP, None),
            P(DP, None),
            P(),
            P(),
        ),
        check_vma=False,
    )
```

profile of v0, /device:TPU:1, one launch (start us, length us, event | category | flops | bytes accessed | tf_op | source)
XLA Modules:
  0.0 401.8 jit_solution(15405271870558576806)
XLA Ops:
  2.4 21.7 %all-to-all-start.6 = ((bf16[64,10,320]{2,1,0:T(8,128)(2,1)}), bf16[64,10,320]{2,1,0:T(8,128)(2,1)S(1)}, u32[]{:S(2)}, u32[]{:S(2)}) async-start(bf16[64,10,320]{2,1,0:T(8,128)(2,1)} %broadcast_in_dim.22), calls=%async_computation.6 | async-start | bytes 1572864 | tf_op jit(solution)/shard_map/all_to_all | solution.py:21
  24.2 40.3 %all-to-all-done.6 = bf16[64,10,320]{2,1,0:T(8,128)(2,1)S(1)} async-done(((bf16[64,10,320]{2,1,0:T(8,128)(2,1)}), bf16[64,10,320]{2,1,0:T(8,128)(2,1)S(1)}, u32[]{:S(2)}, u32[]{:S(2)}) %all-to-all-start.6) | async-done | bytes 409632 | tf_op jit(solution)/shard_map/all_to_all | solution.py:21
  65.5 9.3 %all-to-all-start.4 = ((bf16[64,5,640]{2,1,0:T(8,128)(2,1)}), bf16[64,5,640]{2,1,0:T(8,128)(2,1)S(1)}, u32[]{:S(2)}, u32[]{:S(2)}) async-start(bf16[64,5,640]{2,1,0:T(8,128)(2,1)} %broadcast_in_dim.20), calls=%async_computation.4 | async-start | bytes 1310720 | tf_op jit(solution)/shard_map/all_to_all | solution.py:21
  74.9 21.6 %all-to-all-done.4 = bf16[64,5,640]{2,1,0:T(8,128)(2,1)S(1)} async-done(((bf16[64,5,640]{2,1,0:T(8,128)(2,1)}), bf16[64,5,640]{2,1,0:T(8,128)(2,1)S(1)}, u32[]{:S(2)}, u32[]{:S(2)}) %all-to-all-start.4) | async-done | bytes 409632 | tf_op jit(solution)/shard_map/all_to_all | solution.py:21
  97.7 11.0 %all-to-all-start.7 = ((bf16[2,64,10,320]{3,1,2,0:T(8,128)(2,1)}), bf16[2,64,10,320]{3,1,2,0:T(8,128)(2,1)S(1)}, u32[]{:S(2)}, u32[]{:S(2)}) async-start(bf16[2,64,10,320]{3,1,2,0:T(8,128)(2,1)} %broadcast_in_dim.23), calls=%async_computation.7 | async-start | bytes 1966080 | tf_op jit(solution)/shard_map/all_to_all | solution.py:21
  108.7 1.7 all-to-all-done.7
  110.4 5.2 %all_to_all.65 = bf16[2,64,5,640]{3,1,2,0:T(8,128)(2,1)} all-to-all(bf16[2,64,5,640]{3,1,2,0:T(8,128)(2,1)S(1)} %broadcast_in_dim.21), channel_id=1, replica_groups=mesh['dp_0'=4,'dp_1'=4,'dp_2'=4,'dp_3'=2,'rep'=4] {'dp_3'}, dimensions={0} | all-to-all | bytes 1638400 | tf_op jit(solution)/shard_map/all_to_all | solution.py:21
  116.5 19.1 %all-to-all-start = ((bf16[64,5,640]{2,1,0:T(8,128)(2,1)}), bf16[64,5,640]{2,1,0:T(8,128)(2,1)}, u32[]{:S(2)}, u32[]{:S(2)}) async-start(bf16[64,5,640]{2,1,0:T(8,128)(2,1)} %broadcast_in_dim.16), calls=%async_computation | async-start | bytes 1310720 | tf_op jit(solution)/shard_map/all_to_all | solution.py:21
  137.1 1.6 copy.69
  139.9 1.7 fusion.21
  142.0 18.0 %all-to-all-done = bf16[64,5,640]{2,1,0:T(8,128)(2,1)} async-done(((bf16[64,5,640]{2,1,0:T(8,128)(2,1)}), bf16[64,5,640]{2,1,0:T(8,128)(2,1)}, u32[]{:S(2)}, u32[]{:S(2)}) %all-to-all-start) | async-done | bytes 409632 | tf_op jit(solution)/shard_map/all_to_all | solution.py:21
  161.2 8.9 %all_to_all.66 = bf16[2,64,5,640]{3,1,2,0:T(8,128)(2,1)} all-to-all(bf16[2,64,5,640]{3,1,2,0:T(8,128)(2,1)S(1)} %broadcast_in_dim.17), channel_id=1, replica_groups=mesh['dp_0'=4,'dp_1'=4,'dp_2'=4,'dp_3'=2,'rep'=4] {'dp_3'}, dimensions={0} | all-to-all | bytes 1638400 | tf_op jit(solution)/shard_map/all_to_all | solution.py:21
  171.0 5.5 %all-to-all-start.2 = ((bf16[64,10,320]{2,1,0:T(8,128)(2,1)}), bf16[64,10,320]{2,1,0:T(8,128)(2,1)}, u32[]{:S(2)}, u32[]{:S(2)}) async-start(bf16[64,10,320]{2,1,0:T(8,128)(2,1)} %broadcast_in_dim.18), calls=%async_computation.2 | async-start | bytes 1572864 | tf_op jit(solution)/shard_map/all_to_all | solution.py:21
  176.5 1.6 copy.64
  179.3 1.7 fusion.23
  184.2 1.6 convolution_add_fusion
  185.8 17.0 %all-to-all-done.2 = bf16[64,10,320]{2,1,0:T(8,128)(2,1)} async-done(((bf16[64,10,320]{2,1,0:T(8,128)(2,1)}), bf16[64,10,320]{2,1,0:T(8,128)(2,1)}, u32[]{:S(2)}, u32[]{:S(2)}) %all-to-all-start.2) | async-done | bytes 409632 | tf_op jit(solution)/shard_map/all_to_all | solution.py:21
  202.8 1.2 copy.66
  204.1 6.5 %all_to_all.67 = bf16[2,64,10,320]{3,1,2,0:T(8,128)(2,1)S(1)} all-to-all(bf16[2,64,10,320]{3,1,2,0:T(8,128)(2,1)S(1)} %broadcast_in_dim.19), channel_id=1, replica_groups=mesh['dp_0'=4,'dp_1'=4,'dp_2'=4,'dp_3'=2,'rep'=4] {'dp_3'}, dimensions={0} | all-to-all | bytes 1638400 | tf_op jit(solution)/shard_map/all_to_all | solution.py:21
  215.5 1.3 fusion.12
  220.6 71.1 %all_to_all.68 = bf16[4,2560,80]{1,2,0:T(8,128)(2,1)S(1)} all-to-all(bf16[4,2560,80]{1,2,0:T(8,128)(2,1)S(1)} %bitcast.47), channel_id=1, replica_groups=mesh['dp_0'=4,'dp_1'=4,'dp_2'=4,'dp_3'=2,'rep'=4] {'rep'}, dimensions={0} | all-to-all | bytes 3276800 | tf_op jit(solution)/shard_map/all_to_all | solution.py:55
  293.4 5.4 %all_to_all.69 = f32[2,64,5,160]{3,1,2,0:T(8,128)S(1)} all-to-all(f32[2,64,5,160]{3,1,2,0:T(8,128)S(1)} %copy.77), channel_id=1, replica_groups=mesh['dp_0'=4,'dp_1'=4,'dp_2'=4,'dp_3'=2,'rep'=4] {'dp_3'}, dimensions={0} | all-to-all | bytes 819200 | tf_op jit(solution)/shard_map/all_to_all | solution.py:70
  300.8 4.3 %all_to_all.70 = f32[2,64,10,80]{3,1,2,0:T(8,128)S(1)} all-to-all(f32[2,64,10,80]{3,1,2,0:T(8,128)S(1)} %copy.74), channel_id=1, replica_groups=mesh['dp_0'=4,'dp_1'=4,'dp_2'=4,'dp_3'=2,'rep'=4] {'dp_3'}, dimensions={0} | all-to-all | bytes 819200 | tf_op jit(solution)/shard_map/all_to_all | solution.py:70
  305.1 4.8 %all-to-all-start.12 = ((f32[64,1,800]{2,1,0:T(1,128)}), f32[64,1,800]{2,1,0:T(1,128)S(1)}, u32[]{:S(2)}, u32[]{:S(2)}) async-start(f32[64,1,800]{2,1,0:T(1,128)} %reshape.89), calls=%async_computation.12 | async-start | bytes 458752 | tf_op jit(solution)/shard_map/all_to_all | solution.py:77
  311.4 18.9 %all-to-all-done.12 = f32[64,1,800]{2,1,0:T(1,128)S(1)} async-done(((f32[64,1,800]{2,1,0:T(1,128)}), f32[64,1,800]{2,1,0:T(1,128)S(1)}, u32[]{:S(2)}, u32[]{:S(2)}) %all-to-all-start.12) | async-done | bytes 204832 | tf_op jit(solution)/shard_map/all_to_all | solution.py:77
  330.3 7.1 %all-to-all-start.10 = ((f32[64,1,800]{2,1,0:T(1,128)}), f32[64,1,800]{2,1,0:T(1,128)S(1)}, u32[]{:S(2)}, u32[]{:S(2)}) async-start(f32[64,1,800]{2,1,0:T(1,128)} %reshape.91), calls=%async_computation.10 | async-start | bytes 458752 | tf_op jit(solution)/shard_map/all_to_all | solution.py:77
  337.4 9.0 %all-reduce.3 = (f32[320]{0:T(512)S(1)}, f32[320]{0:T(512)S(1)}) all-reduce(f32[320]{0:T(512)S(1)} %get-tuple-element.10, f32[320]{0:T(512)S(1)} %get-tuple-element.13), channel_id=1, replica_groups=mesh['dp_0'=4,'dp_1'=4,'dp_2'=4,'dp_3'=2,'rep'=4] {'dp_0'}, use_global_device_ids=true, to_apply=%region_13.14 | all-reduce | flops 640 | bytes 5120 | tf_op jit(solution)/shard_map/psum | solution.py:104
  346.4 9.1 %all-reduce.2 = (f32[320]{0:T(512)S(1)}, f32[320]{0:T(512)S(1)}) all-reduce(f32[320]{0:T(512)S(1)} %get-tuple-element.20, f32[320]{0:T(512)S(1)} %get-tuple-element.21), channel_id=1, replica_groups=mesh['dp_0'=4,'dp_1'=4,'dp_2'=4,'dp_3'=2,'rep'=4] {'dp_1'}, use_global_device_ids=true, to_apply=%region_14.15 | all-reduce | flops 640 | bytes 5120 | tf_op jit(solution)/shard_map/psum | solution.py:104
  355.5 13.7 %all-reduce.1 = (f32[320]{0:T(512)S(1)}, f32[320]{0:T(512)S(1)}) all-reduce(f32[320]{0:T(512)S(1)} %get-tuple-element.18, f32[320]{0:T(512)S(1)} %get-tuple-element.19), channel_id=1, replica_groups=mesh['dp_0'=4,'dp_1'=4,'dp_2'=4,'dp_3'=2,'rep'=4] {'dp_2'}, use_global_device_ids=true, to_apply=%region_15.16 | all-reduce | flops 640 | bytes 5120 | tf_op jit(solution)/shard_map/psum | solution.py:104
  369.2 8.6 %all-reduce.4 = (f32[320]{0:T(512)S(1)}, f32[320]{0:T(512)S(1)}) all-reduce(f32[320]{0:T(512)S(1)} %get-tuple-element.16, f32[320]{0:T(512)S(1)} %get-tuple-element.17), channel_id=1, replica_groups=mesh['dp_0'=4,'dp_1'=4,'dp_2'=4,'dp_3'=2,'rep'=4] {'dp_3'}, use_global_device_ids=true, to_apply=%region_16.17 | all-reduce | flops 640 | bytes 5120 | tf_op jit(solution)/shard_map/psum | solution.py:104
  377.8 8.1 %all-reduce = (f32[320]{0:T(512)S(1)}, f32[320]{0:T(512)S(1)}) all-reduce(f32[320]{0:T(512)S(1)} %get-tuple-element.22, f32[320]{0:T(512)S(1)} %get-tuple-element.23), channel_id=1, replica_groups=mesh['dp_0'=4,'dp_1'=4,'dp_2'=4,'dp_3'=2,'rep'=4] {'rep'}, use_global_device_ids=true, to_apply=%region_17.18 | all-reduce | flops 640 | bytes 5120 | tf_op jit(solution)/shard_map/psum | solution.py:104
  390.2 10.2 %all-gather = f32[4,80,20]{1,2,0:T(8,128)S(1)} all-gather(f32[1,80,20]{1,2,0:T(8,128)S(1)} %maximum_bitcast_fusion), channel_id=1, replica_groups=mesh['dp_0'=4,'dp_1'=4,'dp_2'=4,'dp_3'=2,'rep'=4] {'rep'}, dimensions={0}, use_global_device_ids=true | all-gather | bytes 32000 | tf_op jit(solution)/shard_map/all_gather | solution.py:93
  (147 shorter events, 33.7 us)
Async XLA Ops:
  0.6 23.5 %copy-start.10 = (f32[5,320]{1,0:T(8,128)S(1)}, f32[5,320]{1,0:T(8,128)}, u32[]{:S(2)}) copy-start(f32[5,320]{1,0:T(8,128)} %param.23) | copy-start | bytes 19204
  0.7 23.5 %copy-start.11 = (f32[5,320]{1,0:T(8,128)S(1)}, f32[5,320]{1,0:T(8,128)}, u32[]{:S(2)}) copy-start(f32[5,320]{1,0:T(8,128)} %param.22) | copy-start | bytes 19204
  2.4 62.2 %all-to-all-start.6 = ((bf16[64,10,320]{2,1,0:T(8,128)(2,1)}), bf16[64,10,320]{2,1,0:T(8,128)(2,1)S(1)}, u32[]{:S(2)}, u32[]{:S(2)}) async-start(bf16[64,10,320]{2,1,0:T(8,128)(2,1)} %broadcast_in_dim.22), calls=%async_computation.6 | async-start | bytes 1572864 | tf_op jit(solution)/shard_map/all_to_all | solution.py:21
  24.1 50.6 %copy-start.13 = (f32[5,320]{1,0:T(8,128)S(1)}, f32[5,320]{1,0:T(8,128)}, u32[]{:S(2)}) copy-start(f32[5,320]{1,0:T(8,128)} %param.18) | copy-start | bytes 19204
  24.1 50.6 %copy-start.15 = (f32[5,320]{1,0:T(8,128)S(1)}, f32[5,320]{1,0:T(8,128)}, u32[]{:S(2)}) copy-start(f32[5,320]{1,0:T(8,128)} %param.17) | copy-start | bytes 19204
  65.5 31.1 %all-to-all-start.4 = ((bf16[64,5,640]{2,1,0:T(8,128)(2,1)}), bf16[64,5,640]{2,1,0:T(8,128)(2,1)S(1)}, u32[]{:S(2)}, u32[]{:S(2)}) async-start(bf16[64,5,640]{2,1,0:T(8,128)(2,1)} %broadcast_in_dim.20), calls=%async_computation.4 | async-start | bytes 1310720 | tf_op jit(solution)/shard_map/all_to_all | solution.py:21
  97.7 12.7 %all-to-all-start.7 = ((bf16[2,64,10,320]{3,1,2,0:T(8,128)(2,1)}), bf16[2,64,10,320]{3,1,2,0:T(8,128)(2,1)S(1)}, u32[]{:S(2)}, u32[]{:S(2)}) async-start(bf16[2,64,10,320]{3,1,2,0:T(8,128)(2,1)} %broadcast_in_dim.23), calls=%async_computation.7 | async-start | bytes 1966080 | tf_op jit(solution)/shard_map/all_to_all | solution.py:21
  115.6 20.0 %copy-start.7 = (f32[10,320]{1,0:T(8,128)S(1)}, f32[10,320]{1,0:T(8,128)}, u32[]{:S(2)}) copy-start(f32[10,320]{1,0:T(8,128)} %param.16) | copy-start | bytes 38404
  115.6 20.1 %copy-start.30 = (s32[2]{0:T(128)S(1)}, s32[2]{0:T(128)}, u32[]{:S(2)}) copy-start(s32[2]{0:T(128)} %param.15) | copy-start | bytes 28
  116.5 43.5 %all-to-all-start = ((bf16[64,5,640]{2,1,0:T(8,128)(2,1)}), bf16[64,5,640]{2,1,0:T(8,128)(2,1)}, u32[]{:S(2)}, u32[]{:S(2)}) async-start(bf16[64,5,640]{2,1,0:T(8,128)(2,1)} %broadcast_in_dim.16), calls=%async_computation | async-start | bytes 1310720 | tf_op jit(solution)/shard_map/all_to_all | solution.py:21
  135.8 43.5 %copy-start.18 = (f32[2,320]{1,0:T(2,128)}, f32[2,320]{1,0:T(2,128)S(1)}, u32[]{:S(2)}) copy-start(f32[2,320]{1,0:T(2,128)S(1)} %get-tuple-element.40) | copy-start | bytes 7684
  135.8 43.5 %copy-start.20 = (f32[2,320]{1,0:T(2,128)}, f32[2,320]{1,0:T(2,128)S(1)}, u32[]{:S(2)}) copy-start(f32[2,320]{1,0:T(2,128)S(1)} %get-tuple-element.41) | copy-start | bytes 7684
  171.0 31.7 %all-to-all-start.2 = ((bf16[64,10,320]{2,1,0:T(8,128)(2,1)}), bf16[64,10,320]{2,1,0:T(8,128)(2,1)}, u32[]{:S(2)}, u32[]{:S(2)}) async-start(bf16[64,10,320]{2,1,0:T(8,128)(2,1)} %broadcast_in_dim.18), calls=%async_computation.2 | async-start | bytes 1572864 | tf_op jit(solution)/shard_map/all_to_all | solution.py:21
  179.3 3.0 copy-start.1
  183.0 1.1 copy-start.4
  211.2 1.1 copy-start.2
  211.2 1.2 copy-start.6
  213.7 1.1 copy-start.3
  213.7 1.3 copy-start.5
  298.8 1.4 slice-start
  305.1 25.2 %all-to-all-start.12 = ((f32[64,1,800]{2,1,0:T(1,128)}), f32[64,1,800]{2,1,0:T(1,128)S(1)}, u32[]{:S(2)}, u32[]{:S(2)}) async-start(f32[64,1,800]{2,1,0:T(1,128)} %reshape.89), calls=%async_computation.12 | async-start | bytes 458752 | tf_op jit(solution)/shard_map/all_to_all | solution.py:77
  309.9 76.0 %copy-start.23 = (f32[320]{0:T(512)S(1)}, f32[320]{0:T(512)}, u32[]{:S(2)}) copy-start(f32[320]{0:T(512)} %param.25) | copy-start | bytes 3844
  310.0 76.0 %copy-start.25 = (f32[320]{0:T(512)S(1)}, f32[320]{0:T(512)}, u32[]{:S(2)}) copy-start(f32[320]{0:T(512)} %param.24) | copy-start | bytes 3844
  310.0 76.0 %copy-start.27 = (f32[320]{0:T(512)S(1)}, f32[320]{0:T(512)}, u32[]{:S(2)}) copy-start(f32[320]{0:T(512)} %param.20) | copy-start | bytes 3844
  330.3 58.4 %all-to-all-start.10 = ((f32[64,1,800]{2,1,0:T(1,128)}), f32[64,1,800]{2,1,0:T(1,128)S(1)}, u32[]{:S(2)}, u32[]{:S(2)}) async-start(f32[64,1,800]{2,1,0:T(1,128)} %reshape.91), calls=%async_computation.10 | async-start | bytes 458752 | tf_op jit(solution)/shard_map/all_to_all | solution.py:77
  385.9 4.2 %copy-start.28 = (f32[320]{0:T(512)}, f32[320]{0:T(512)S(1)}, u32[]{:S(2)}) copy-start(f32[320]{0:T(512)S(1)} %get-tuple-element.14) | copy-start | bytes 3844
  385.9 4.2 %copy-start.29 = (f32[320]{0:T(512)}, f32[320]{0:T(512)S(1)}, u32[]{:S(2)}) copy-start(f32[320]{0:T(512)S(1)} %get-tuple-element.15) | copy-start | bytes 3844
  388.4 12.1 %copy-start.8 = (f32[10,320]{1,0:T(8,128)S(1)}, f32[10,320]{1,0:T(8,128)}, u32[]{:S(2)}) copy-start(f32[10,320]{1,0:T(8,128)} %param.16) | copy-start | bytes 38404
  388.4 12.1 %copy-start.9 = (f32[10,320]{1,0:T(8,128)S(1)}, f32[10,320]{1,0:T(8,128)}, u32[]{:S(2)}) copy-start(f32[10,320]{1,0:T(8,128)} %param.21) | copy-start | bytes 38404
  388.4 12.7 %copy-start.12 = (f32[5,320]{1,0:T(8,128)S(1)}, f32[5,320]{1,0:T(8,128)}, u32[]{:S(2)}) copy-start(f32[5,320]{1,0:T(8,128)} %param.22) | copy-start | bytes 19204
  388.4 12.7 %copy-start.14 = (f32[5,320]{1,0:T(8,128)S(1)}, f32[5,320]{1,0:T(8,128)}, u32[]{:S(2)}) copy-start(f32[5,320]{1,0:T(8,128)} %param.18) | copy-start | bytes 19204
  388.5 12.7 %copy-start.16 = (f32[5,320]{1,0:T(8,128)S(1)}, f32[5,320]{1,0:T(8,128)}, u32[]{:S(2)}) copy-start(f32[5,320]{1,0:T(8,128)} %param.17) | copy-start | bytes 19204
  (7 other events, 5.6 us)
where the time goes:
time: 405 us; the launch traced here: 402 us
  blocking collectives  160 us (40%)
  waiting for transfers between devices  117 us (29%)
  starting transfers between devices  78.5 us (19%)
  local copies, waits for them, and re-layouts  25.5 us (6%)
  matrix products  11.3 us (3%)
  other arithmetic  7.63 us (2%)
    all_to_all x5, waiting for transfers between devices, copy_for_each(): lax.all_to_all(jnp.broadcast_to(shard[None], (peers, *shard.shape)), axis...  98.6 us
    all_to_all x1, blocking collectives, sum_at_owner(): tiles = lax.all_to_all(cut_along(shard, dim, peers), axis, 0, 0, tiled=True)  71.1 us
    all_to_all x5, starting transfers between devices, copy_for_each(): lax.all_to_all(jnp.broadcast_to(shard[None], (peers, *shard.shape)), axis...  66.5 us
    psum x5, blocking collectives, by_axis(): return functools.reduce(lax.psum, axes, shard)  48.5 us
    all_to_all x3, blocking collectives, copy_for_each(): lax.all_to_all(jnp.broadcast_to(shard[None], (peers, *shard.shape)), axis...  20.5 us
    all_to_all x2, waiting for transfers between devices, sum_by_axis(): return jnp.sum(lax.all_to_all(own, far, 0, 0, tiled=True), axis=0)  18.9 us
    all_to_all x2, starting transfers between devices, sum_by_axis(): return jnp.sum(lax.all_to_all(own, far, 0, 0, tiled=True), axis=0)  12 us
    all_gather x1, blocking collectives, rows_first(): whole = lax.all_gather(both, axis, axis=0, tiled=True)  10.2 us
  transfers between devices with their start and end apart: 7, of which 6 were waited for; matrix products, arithmetic and copies ran while one was open for 5% of the time, Pallas kernels for 0%

commit v1 on v0

v1 whole, which is shorter than its diff:
```python
import functools
import math

import jax
import jax.numpy as jnp
import numpy as np
from jax import lax
from jax.experimental import pallas as pl
from jax.experimental.pallas import tpu as pltpu
from jax.sharding import Mesh
from jax.sharding import PartitionSpec as P

SKIP = 20
DP = ("x", "y", "zh", "core")
DP_REP = ("x", "y", "zh", "core", "zl")
EMA_DECAY = 0.95
LEARN_RATE = 0.05
F32, BF16 = jnp.float32, jnp.bfloat16
VMEM = pl.BlockSpec(memory_space=pltpu.VMEM)


def here():
    return tuple(lax.axis_index(a) for a in ("x", "y", "zh", "core", "zl"))


def send(src, dst, send_sem, recv_sem, device):
    copy = pltpu.make_async_remote_copy(
        src_ref=src,
        dst_ref=dst,
        send_sem=send_sem,
        recv_sem=recv_sem,
        device_id=device,
        device_id_type=pl.DeviceIdType.MESH,
    )
    copy.start()
    return copy


def greet(device):
    pl.semaphore_signal(
        pltpu.get_barrier_semaphore(), inc=1, device_id=device, device_id_type=pl.DeviceIdType.MESH
    )


class Sender:
    def __init__(self, send_sems, recv_sems):
        self.send_sems, self.recv_sems, self.started = send_sems, recv_sems, []

    def __call__(self, src, dst, device):
        at = len(self.started)
        copy = send(src, dst, self.send_sems.at[at], self.recv_sems.at[at], device)
        self.started.append(copy)
        return copy

    def finish(self):
        for copy in self.started:
            copy.wait_send()


def along(first, k, x, y, c):
    on_x = (1 - c) if first else c
    return {"x": (x + on_x * k) % 4, "y": (y + (1 - on_x) * k) % 4}


def block(k, m, x, y, c):
    return ((x + (1 - c) * k + c * m) % 4) * 4 + (y + c * k + (1 - c) * m) % 4


G_COPIES = 8 + 4 + 12 + 15


def gather_kernel(pack, sel, out, zbuf, send_sems, recv_sems):
    x, y, zh, c, zl = here()
    other = {"core": 1 - c}
    ahead, behind = {"zh": (zh + 1) % 4}, {"zh": (zh + 3) % 4}
    first_on, first_back = along(True, 1, x, y, c), along(True, 3, x, y, c)
    second_on, second_back = along(False, 1, x, y, c), along(False, 3, x, y, c)
    for device in (other, ahead, behind, first_on, first_back, second_on, second_back):
        greet(device)
    pl.semaphore_wait(pltpu.get_barrier_semaphore(), 7)
    go = Sender(send_sems, recv_sems)

    def slot(k):
        return pl.ds(pl.multiple_of((((zh + k) % 4) * 2 + c) * 32, 32), 32)

    zbuf[slot(0), :] = pack[...]
    mine = zbuf.at[slot(0), :]
    from_behind = go(pack, mine, ahead)
    from_ahead = go(pack, mine, behind)
    shared = [go(pack, mine, other)]
    from_behind.wait_recv()
    held = zbuf.at[slot(3), 0:384]
    part_on = go(held, held, ahead)
    held = zbuf.at[slot(3), :]
    shared.append(go(held, held, other))
    from_ahead.wait_recv()
    held = zbuf.at[slot(1), 384:640]
    part_back = go(held, held, behind)
    held = zbuf.at[slot(1), :]
    shared.append(go(held, held, other))
    part_on.wait_recv()
    part_back.wait_recv()
    held = zbuf.at[slot(2), :]
    shared.append(go(held, held, other))
    for copy in shared:
        copy.wait_recv()

    rows = jnp.dot(sel[...], zbuf[...], preferred_element_type=F32).astype(BF16)
    at = x * 4 + y
    out[0, at] = rows[0:80]
    out[1, at] = rows[80:160]

    def held_block(k, m):
        return out.at[c, block(k, m, x, y, c)]

    crossed = []

    def pass_on(k):
        b = held_block(k, 0)
        return (go(b, b, second_on), go(b, b, second_back))

    def across(k, m):
        b = held_block(k, m)
        crossed.append(go(b, b, other))

    own = held_block(0, 0)
    from_back = go(own, own, first_on)
    from_on = go(own, own, first_back)
    seconds = {0: pass_on(0)}
    from_back.wait_recv()
    b = out.at[c, block(3, 0, x, y, c), :, 0:384]
    part_on = go(b, b, first_on)
    seconds[3] = pass_on(3)
    across(3, 0)
    from_on.wait_recv()
    b = out.at[c, block(1, 0, x, y, c), :, 384:640]
    part_back = go(b, b, first_back)
    seconds[1] = pass_on(1)
    across(1, 0)
    relays = []
    for k in (0, 3, 1, 2):
        if k == 2:
            part_on.wait_recv()
            part_back.wait_recv()
            seconds[2] = pass_on(2)
            across(2, 0)
        seconds[k][0].wait_recv()
        if k in (0, 1):
            b = held_block(k, 3)
            relays.append((k, go(b, b, second_on)))
        across(k, 3)
        seconds[k][1].wait_recv()
        if k in (3, 2):
            b = held_block(k, 1)
            relays.append((k, go(b, b, second_back)))
        across(k, 1)
    for k, copy in relays:
        copy.wait_recv()
        across(k, 2)
    for copy in crossed:
        copy.wait_recv()
    go.finish()


def gather(pack, sel):
    return pl.pallas_call(
        gather_kernel,
        out_shape=jax.ShapeDtypeStruct((2, 16, 80, 640), BF16),
        in_specs=[VMEM, VMEM],
        out_specs=VMEM,
        scratch_shapes=[
            pltpu.VMEM((256, 640), BF16),
            pltpu.SemaphoreType.DMA((G_COPIES,)),
            pltpu.SemaphoreType.DMA((G_COPIES,)),
        ],
        compiler_params=pltpu.CompilerParams(collective_id=0, has_side_effects=True),
        name="gather",
    )(pack, sel)


def contract_last(left, right):
    return lax.dot_general(left, right, (((1,), (1,)), ((), ())), preferred_element_type=F32)


def contract_first(left, right):
    return lax.dot_general(left, right, (((0,), (0,)), ((), ())), preferred_element_type=F32)


def compute_kernel(
    s_in, t_in, vecs, feats, feats_t, w, grads, sums, emb, emb_grad, w_out, normed_s, mix_s, hidden_s, grad_s
):
    lane = lax.broadcasted_iota(jnp.int32, (1, 384), 1)
    in_s, in_t = lane < 320, lane >= 64
    for i in range(8):
        a = w[1, 2 * i].astype(F32)[0:40]
        b = w[1, 2 * i + 1].astype(F32)[0:40]
        w_out[80 * i : 80 * i + 80, :] = jnp.concatenate([a, b], axis=0).astype(BF16)
    rest = w[1].reshape(1280, 640)
    emb[...] = jnp.dot(feats[...], rest, preferred_element_type=F32)

    def forward(tokens, shift, gain, bias, inside, lanes):
        summed = jnp.where(inside, tokens.astype(F32) + shift, 0.0)
        mean = jnp.sum(summed, axis=1, keepdims=True) / 320
        center = jnp.where(inside, summed - mean, 0.0)
        inv_std = lax.rsqrt(jnp.sum(center * center, axis=1, keepdims=True) / 320 + 1e-05)
        normed = center * inv_std
        normed_b = (normed * gain + bias).astype(BF16)
        mixed = contract_last(normed_b, w[0, :, :, lanes].reshape(1280, 384))
        gate, up = mixed[:, :640], mixed[:, 640:]
        tangent = jnp.tanh(0.7978845608 * (gate + 0.044715 * gate * gate * gate))
        gelu = 0.5 * gate * (1.0 + tangent)
        hidden = (gelu * up).astype(BF16)
        out = summed + jnp.dot(hidden, w_out[:, lanes], preferred_element_type=F32)
        return out, normed, inv_std, normed_b, gate, up, tangent, gelu, hidden

    sums[...] = jnp.zeros_like(sums)

    def one_sample(s, _):
        rows = pl.ds(pl.multiple_of(s * 256, 256), 256)
        zeros = jnp.zeros((256, 64), BF16)
        t = t_in[rows, :]
        tokens_t = jnp.concatenate([zeros, t[:, 256:320], t[:, 0:256]], axis=1)
        out_t = forward(
            tokens_t, emb[pl.ds(2 + s, 1), 256:640], vecs[2:3, :], vecs[3:4, :], in_t, slice(256, 640)
        )[0]
        tokens_s = jnp.concatenate([s_in[rows, :], zeros], axis=1)
        gain = vecs[0:1, :]
        out_s, normed, inv_std, normed_b, gate, up, tangent, gelu, hidden = forward(
            tokens_s, emb[pl.ds(s, 1), 0:384], gain, vecs[1:2, :], in_s, slice(0, 384)
        )
        turned = jnp.concatenate(
            [out_t[:, 128:384], pltpu.roll(out_t[:, 0:128], 64, axis=1)], axis=1
        )
        grad_y = jnp.where(in_s, (out_s - turned) / 512, 0.0)
        grad_yb = grad_y.astype(BF16)
        grad_h = contract_last(grad_yb, w_out[:, 0:384])
        slope = 0.5 * (1.0 + tangent) + 0.5 * gate * (1.0 - tangent * tangent) * 0.7978845608 * (
            1.0 + 0.134145 * gate * gate
        )
        grad_mix = jnp.concatenate(
            [(grad_h * up * slope).astype(BF16), (grad_h * gelu).astype(BF16)], axis=1
        )
        grad_z = jnp.dot(grad_mix, w[0, :, :, 0:384].reshape(1280, 384), preferred_element_type=F32)
        grad_z = jnp.where(in_s, grad_z, 0.0)
        sums[0, 0:1, :] += jnp.sum(grad_z * normed, axis=0, keepdims=True)
        sums[1, 0:1, :] += jnp.sum(grad_z, axis=0, keepdims=True)
        grad_n = grad_z * gain
        mean_n = jnp.sum(grad_n, axis=1, keepdims=True) / 320
        mean_nn = jnp.sum(grad_n * normed, axis=1, keepdims=True) / 320
        grad_sum = grad_y + inv_std * (grad_n - mean_n - normed * mean_nn)
        grad_sum = jnp.where(in_s, grad_sum, 0.0)
        emb_grad[pl.ds(s, 1), :] = jnp.sum(grad_sum, axis=0, keepdims=True)
        normed_s[rows, :] = normed_b
        mix_s[rows, :] = grad_mix
        hidden_s[rows, :] = hidden
        grad_s[rows, :] = grad_yb
        return 0

    lax.fori_loop(0, 2, one_sample, 0)
    full_in = contract_first(mix_s[...], normed_s[...])
    grads[0] = full_in.astype(BF16).reshape(16, 80, 384)
    full_out = contract_first(hidden_s[...], grad_s[...])
    full_time = feats_t[:, 0:1] * emb_grad[0:1, :] + feats_t[:, 1:2] * emb_grad[1:2, :]
    for b in range(16):
        r = slice(40 * b, 40 * b + 40)
        grads[1, b] = jnp.concatenate([full_out[r], full_time[r]], axis=0).astype(BF16)


def compute(s_in, t_in, vecs, feats, feats_t, w):
    return pl.pallas_call(
        compute_kernel,
        out_shape=(
            jax.ShapeDtypeStruct((2, 16, 80, 384), BF16),
            jax.ShapeDtypeStruct((2, 8, 384), F32),
        ),
        in_specs=[VMEM] * 6,
        out_specs=(VMEM, VMEM),
        scratch_shapes=[
            pltpu.VMEM((8, 640), F32),
            pltpu.VMEM((8, 384), F32),
            pltpu.VMEM((640, 640), BF16),
            pltpu.VMEM((512, 384), BF16),
            pltpu.VMEM((512, 1280), BF16),
            pltpu.VMEM((512, 640), BF16),
            pltpu.VMEM((512, 384), BF16),
        ],
        compiler_params=pltpu.CompilerParams(vmem_limit_bytes=60 * 2**20),
        name="step",
    )(s_in, t_in, vecs, feats, feats_t, w)


R_COPIES = 17 + 4 + 8 + 3 + 2 + 2 + 3 + 6


def reduce_kernel(
    grads, sums, spread, out, total, part, acc, early, from_back, from_on, mids, early_2, back_2, on_2,
    zblk, quarters, fin, vd, va, vb, vz, vfin, vown, owned, send_sems, recv_sems, far_send, far_recv,
):
    x, y, zh, c, zl = here()
    other = {"core": 1 - c}
    first_on, first_back = along(True, 1, x, y, c), along(True, 3, x, y, c)
    second_on, second_back = along(False, 1, x, y, c), along(False, 3, x, y, c)
    first_far, second_far = along(True, 2, x, y, c), along(False, 2, x, y, c)
    rep_peers = [{"zl": (zl + k) % 4} for k in (1, 2, 3)]
    near = [other, first_on, first_back, first_far, second_on, second_back, second_far] + rep_peers
    for device in near:
        greet(device)
    for h in range(4):
        for k in range(2):
            itself = (zl == zh) & (h == zh) & (k == c)

            @pl.when(jnp.logical_not(itself))
            def _():
                greet({"zh": h, "zl": zh, "core": k})

    barrier = pltpu.get_barrier_semaphore()
    pl.semaphore_wait(barrier, jnp.where(zl == zh, len(near) + 7, len(near) + 8))

    go = Sender(send_sems, recv_sems)
    pairs = [(k, m) for k in (2, 1, 3, 0) for m in range(4)]
    crossed = {}
    for k, m in pairs:
        b = block(k, m, x, y, 1 - c)
        crossed[k, m] = go(grads.at[1 - c, b], part.at[k * 4 + m], other)
    vec_in = go(sums.at[1 - c], vd, other)

    def local(k, m):
        crossed[k, m].wait_recv()
        b = block(k, m, x, y, c)
        return grads[c, b].astype(F32) + part[k * 4 + m].astype(F32)

    relay = {}
    for m in range(4):
        acc[8 + m] = local(2, m).astype(BF16)
        relay[m] = go(acc.at[8 + m], early.at[m], first_on if m < 2 else first_back)
    arrive_back, arrive_on = {}, {}
    for m in (2, 3):
        acc[4 + m] = local(1, m).astype(BF16)
        arrive_back[m] = go(acc.at[4 + m], from_back.at[m], first_on)
    for m in (0, 1):
        acc[12 + m] = local(3, m).astype(BF16)
        arrive_on[m] = go(acc.at[12 + m], from_on.at[m], first_back)

    vec_in.wait_recv()
    own = jnp.where(c == 0, x, y)
    va[own] = sums[c] + vd[...]
    vown[0] = va[own]
    vec_a = [go(vown.at[0], va.at[own], along(True, k, x, y, c)) for k in (1, 2, 3)]

    for m in (0, 1):
        mine = local(1, m)
        relay[m].wait_recv()
        acc[4 + m] = (mine + early[m].astype(F32)).astype(BF16)
        arrive_back[m] = go(acc.at[4 + m], from_back.at[m], first_on)
    for m in (2, 3):
        mine = local(3, m)
        relay[m].wait_recv()
        acc[12 + m] = (mine + early[m].astype(F32)).astype(BF16)
        arrive_on[m] = go(acc.at[12 + m], from_on.at[m], first_back)

    for copy in vec_a:
        copy.wait_recv()
    own_2 = jnp.where(c == 0, y, x)
    vb[own_2] = ((va[0] + va[1]) + va[2]) + va[3]
    vown[1] = vb[own_2]
    vec_b = [go(vown.at[1], vb.at[own_2], along(False, k, x, y, c)) for k in (1, 2, 3)]

    def first_sum(m):
        mine = local(0, m)
        arrive_back[m].wait_recv()
        arrive_on[m].wait_recv()
        return mine + from_back[m].astype(F32) + from_on[m].astype(F32)

    mids[2] = first_sum(2).astype(BF16)
    up = go(mids.at[2, 0:48], early_2.at[0:48], second_on)
    down = go(mids.at[2, 48:80], early_2.at[48:80], second_back)
    mine_1, mine_3 = first_sum(1), first_sum(3)
    up.wait_recv()
    mids[1, 0:48] = (mine_1[0:48] + early_2[0:48].astype(F32)).astype(BF16)
    mids[1, 48:80] = mine_1[48:80].astype(BF16)
    last_back = go(mids.at[1], back_2, second_on)
    down.wait_recv()
    mids[3, 0:48] = mine_3[0:48].astype(BF16)
    mids[3, 48:80] = (mine_3[48:80] + early_2[48:80].astype(F32)).astype(BF16)
    last_on = go(mids.at[3], on_2, second_back)
    mine_0 = first_sum(0)

    for copy in vec_b:
        copy.wait_recv()
    vz[zl] = ((vb[0] + vb[1]) + vb[2]) + vb[3]
    vown[2] = vz[zl]
    vec_z = [go(vown.at[2], vz.at[zl], device) for device in rep_peers]

    last_back.wait_recv()
    last_on.wait_recv()
    plane = (mine_0 + back_2[...].astype(F32) + on_2[...].astype(F32)).astype(BF16)
    zblk[...] = jnp.dot(spread[c], plane, preferred_element_type=F32).astype(BF16).reshape(8, 16, 384)
    quarters[zl] = zblk[pl.ds(2 * zl, 2)]
    rep_in = []
    for k in (1, 2, 3):
        j = (zl + k) % 4
        rep_in.append(go(zblk.at[pl.ds(2 * j, 2)], quarters.at[zl], {"zl": j}))
    for copy in rep_in:
        copy.wait_recv()
    q = [quarters[j].astype(F32) for j in range(4)]
    owned[...] = (((q[0] + q[1]) + q[2]) + q[3]).astype(BF16)
    for copy in vec_z:
        copy.wait_recv()
    vown[3] = ((vz[0] + vz[1]) + vz[2]) + vz[3]

    me = zh * 2 + c
    for j in range(4):
        for k in range(2):
            itself = (zl == zh) & (j == zl) & (k == c)
            at = j * 2 + k
            device = {"zh": zl, "zl": j, "core": k}

            @pl.when(jnp.logical_not(itself))
            def _():
                send(owned.at[k], fin.at[me], far_send.at[at], far_recv.at[me], device)
                send(vown.at[3], vfin.at[me], far_send.at[8 + at], far_recv.at[8 + me], device)

    @pl.when(zl == zh)
    def _():
        fin[me] = owned[c]
        vfin[me] = vown[3]

    def far(at, src, dst, recv):
        return pltpu.make_async_remote_copy(
            src_ref=src, dst_ref=dst, send_sem=far_send.at[at], recv_sem=far_recv.at[recv],
            device_id=other, device_id_type=pl.DeviceIdType.MESH,
        )

    for h in range(4):
        for k in range(2):
            at = h * 2 + k
            itself = (zl == zh) & (h == zh) & (k == c)

            @pl.when(jnp.logical_not(itself))
            def _():
                far(at, owned.at[0], fin.at[at], at).wait_recv()
                far(8 + at, vown.at[3], vfin.at[at], 8 + at).wait_recv()

    for k in range(2):
        f = [fin[2 * h + k].astype(F32) for h in range(4)]
        out[k] = ((f[0] + f[1]) + f[2]) + f[3]
        total[k] = ((vfin[k] + vfin[2 + k]) + vfin[4 + k]) + vfin[6 + k]
    go.finish()
    for j in range(4):
        for k in range(2):
            itself = (zl == zh) & (j == zl) & (k == c)
            at = j * 2 + k

            @pl.when(jnp.logical_not(itself))
            def _():
                far(at, owned.at[0], fin.at[at], at).wait_send()
                far(8 + at, vown.at[3], vfin.at[at], 8 + at).wait_send()


def reduce(grads, sums, spread):
    return pl.pallas_call(
        reduce_kernel,
        out_shape=(
            jax.ShapeDtypeStruct((2, 16, 384), F32),
            jax.ShapeDtypeStruct((2, 8, 384), F32),
        ),
        in_specs=[VMEM] * 3,
        out_specs=(VMEM, VMEM),
        scratch_shapes=[
            pltpu.VMEM((16, 80, 384), BF16),
            pltpu.VMEM((16, 80, 384), BF16),
            pltpu.VMEM((4, 80, 384), BF16),
            pltpu.VMEM((4, 80, 384), BF16),
            pltpu.VMEM((4, 80, 384), BF16),
            pltpu.VMEM((4, 80, 384), BF16),
            pltpu.VMEM((80, 384), BF16),
            pltpu.VMEM((80, 384), BF16),
            pltpu.VMEM((80, 384), BF16),
            pltpu.VMEM((8, 16, 384), BF16),
            pltpu.VMEM((4, 2, 16, 384), BF16),
            pltpu.VMEM((8, 16, 384), BF16),
            pltpu.VMEM((8, 384), F32),
            pltpu.VMEM((4, 8, 384), F32),
            pltpu.VMEM((4, 8, 384), F32),
            pltpu.VMEM((4, 8, 384), F32),
            pltpu.VMEM((8, 8, 384), F32),
            pltpu.VMEM((4, 8, 384), F32),
            pltpu.VMEM((2, 16, 384), BF16),
            pltpu.SemaphoreType.DMA((R_COPIES,)),
            pltpu.SemaphoreType.DMA((R_COPIES,)),
            pltpu.SemaphoreType.DMA((16,)),
            pltpu.SemaphoreType.DMA((16,)),
        ],
        compiler_params=pltpu.CompilerParams(collective_id=1, has_side_effects=True),
        name="reduce",
    )(grads, sums, spread)


def selection():
    sel = np.zeros((160, 256), np.float32)
    spread = np.zeros((2, 128, 80), np.float32)
    for d in range(8):
        for r in range(10):
            sel[d * 10 + r, d * 32 + r] = 1
            spread[0, d * 16 + r, d * 10 + r] = 1
        for r in range(5):
            sel[80 + d * 5 + r, d * 32 + 10 + r] = 1
            sel[120 + d * 5 + r, d * 32 + 15 + r] = 1
            spread[1, d * 16 + r, d * 5 + r] = 1
            spread[1, d * 16 + 5 + r, 40 + d * 5 + r] = 1
    return jnp.asarray(sel, BF16), jnp.asarray(spread, BF16)


def sinusoid(step_ids, width, order):
    half_width = width // 2
    frequency = jnp.exp(-math.log(10000.0) * (order % half_width).astype(F32) / half_width)
    angles = step_ids.astype(F32)[:, None] * frequency[None, :]
    wave = jnp.where(order[None, :] < half_width, jnp.cos(angles), jnp.sin(angles))
    return jax.nn.silu(wave)


def per_device(
    student_in, target_in, timesteps,
    student_win, student_wout, student_wtime, student_gain, student_bias,
    target_win, target_wout, target_wtime, target_gain, target_bias,
):
    sel, spread = selection()
    rows_s = jnp.concatenate([student_win, student_wout, student_wtime], axis=0)
    rows_t = jnp.concatenate([target_win, target_wout, target_wtime], axis=0)
    pack = jnp.concatenate([rows_s, rows_t[:, 256:], rows_t[:, :256]], axis=1).astype(BF16)
    pack = jnp.pad(pack, ((0, 12), (0, 0)))
    weights = gather(pack, sel)

    spot = jnp.arange(1280, dtype=jnp.int32)
    order = (spot // 80) * 40 + spot % 80 - 40
    steps = jnp.concatenate([timesteps, timesteps - SKIP])
    feats = jnp.where(spot[None, :] % 80 >= 40, sinusoid(steps, 640, order), 0.0)
    feats = jnp.pad(feats.astype(BF16), ((0, 4), (0, 0)))
    plain = sinusoid(timesteps, 640, jnp.arange(640, dtype=jnp.int32)).astype(BF16)
    feats_t = plain.astype(F32).T
    student = jnp.pad(jnp.stack([student_gain, student_bias]), ((0, 0), (0, 64)))
    target = jnp.stack([target_gain, target_bias])
    target = jnp.concatenate([jnp.zeros((2, 64), F32), target[:, 256:], target[:, :256]], axis=1)
    vecs = jnp.concatenate([student, target, jnp.zeros((4, 384), F32)], axis=0)
    grads, sums = compute(student_in, target_in, vecs, feats, feats_t, weights)
    owned, totals = reduce(grads, sums, spread)
    grad_win = owned[0, :10, :320]
    grad_wout = owned[1, :5, :320]
    grad_wtime = owned[1, 5:10, :320]
    grad_gain, grad_bias = totals[0, 0, :320], totals[1, 0, :320]

    def average(target_p, student_p, grad_p):
        return EMA_DECAY * target_p + (1.0 - EMA_DECAY) * (student_p - LEARN_RATE * grad_p)

    return (
        grad_win, grad_wout, grad_wtime, grad_gain, grad_bias,
        average(target_win, student_win, grad_win),
        average(target_wout, student_wout, grad_wout),
        average(target_wtime, student_wtime, grad_wtime),
        average(target_gain, student_gain, grad_gain),
        average(target_bias, student_bias, grad_bias),
    )


def solution(mesh):
    split = Mesh(mesh.devices.reshape(4, 4, 4, 2, 4), DP_REP)
    row, vec, tok = P(DP, None), P(), P(DP_REP, None)
    return jax.shard_map(
        per_device,
        mesh=split,
        in_specs=(tok, tok, P(DP_REP), row, row, row, vec, vec, row, row, row, vec, vec),
        out_specs=(row, row, row, vec, vec, row, row, row, vec, vec),
        check_vma=False,
    )
```

time: 405 us -> 120 us (0.30)
  blocking collectives: 160 us -> 0 us
  waiting for transfers between devices: 117 us -> 0 us
  Pallas kernels: 0 us -> 95.8 us
  starting transfers between devices: 78.5 us -> 0 us
  local copies, waits for them, and re-layouts: 25.5 us -> 8.07 us
  matrix products: 11.3 us -> 0 us
  other arithmetic: 7.63 us -> 13.1 us
    all_to_all x7 -> x0, waiting for transfers between devices: 117 us -> none  [the longest x5 98.6 us: copy_for_each(): lax.all_to_all(jnp.broadcast_to(shard[None], (peers, *shard.shape)), axis...]
    all_to_all x6 -> x0, blocking collectives: 101 us -> none  [the longest x1 71.1 us: sum_at_owner(): tiles = lax.all_to_all(cut_along(shard, dim, peers), axis, 0, 0, tiled=True)]
    pallas_call x0 -> x3, Pallas kernels: none -> 95.8 us  [the longest x1 50 us: gather(): pl.pallas_call(gather_kernel, out_shape=jax.ShapeDtypeStruct((2, 16, 80,...]
    all_to_all x7 -> x0, starting transfers between devices: 78.5 us -> none  [the longest x5 66.5 us: copy_for_each(): lax.all_to_all(jnp.broadcast_to(shard[None], (peers, *shard.shape)), axis...]
    psum x5 -> x0, blocking collectives: 48.5 us -> none  [by_axis(): return functools.reduce(lax.psum, axes, shard)]
    dot_general x11 -> x0, matrix products: 11.3 us -> none  [the longest x2 3.36 us: forward(): embedding = jnp.dot(time_feat, w_time, preferred_element_type=jnp.float32)]
    all_gather x1 -> x0, blocking collectives: 10.2 us -> none  [rows_first(): whole = lax.all_gather(both, axis, axis=0, tiled=True)]
    transpose x7 -> x0, local copies, waits for them, and re-layouts: 5.37 us -> none  [the longest x4 4.53 us: gathered_by_axis(): tiles = jnp.swapaxes(copy_for_each(initial, near), 0, 1)]
  transfers between devices with their start and end apart: 7 -> 0, of which waited for: 6 -> 0; matrix products, arithmetic and copies ran while one was open for 5% -> 0% of each run, Pallas kernels for 0% -> 0%
where the time goes in v1:
time: 120 us; the launch traced here: 118 us
  Pallas kernels  95.8 us (80%)
  other arithmetic  13.1 us (11%)
  local copies, waits for them, and re-layouts  8.07 us (7%)
    pallas_call x1, Pallas kernels, gather(): pl.pallas_call(gather_kernel, out_shape=jax.ShapeDtypeStruct((2, 16, 80,...  50 us
    pallas_call x1, Pallas kernels, reduce(): pl.pallas_call(reduce_kernel, out_shape=(jax.ShapeDtypeStruct((2, 16, 384...  35.5 us
    pallas_call x1, Pallas kernels, compute(): pl.pallas_call(compute_kernel, out_shape=(jax.ShapeDtypeStruct((2, 16, 80...  10.4 us
    add x4, other arithmetic, average(): EMA_DECAY * target_p + (1.0 - EMA_DECAY) * (student_p - LEARN_RATE * grad_p)  3.93 us
    unnamed x26, local copies, waits for them, and re-layouts  3.89 us
    another operation x4, other arithmetic  2.92 us

profile of v1, /device:TPU:1, one launch (start us, length us, event | category | flops | bytes accessed | tf_op | source)
XLA Modules:
  0.0 117.8 jit_solution(17391930074806837370)
XLA Ops:
  0.7 0.1 pad.29.clone
  0.7 0.7 fusion.44
  1.5 0.7 add_convert_fusion
  2.2 0.7 stack.18
  2.9 0.7 stack.19
  3.6 0.7 stack.21
  4.3 0.7 stack.22
  5.0 0.7 fusion.21.vecs
  5.7 0.7 convert.17
  6.4 0.7 convert.18
  7.1 0.7 maximum_convert_fusion
  7.9 0.3 select_convert_fusion
  8.1 0.6 pad.13.feats
  8.7 0.7 convert.16
  9.5 0.8 fusion.17
  10.3 0.7 fusion.16.pack
  10.9 2.3 %fusion.7.feats_t = f32[640,2]{1,0:T(8,128)} fusion(f32[640]{0:T(1024)S(1)} %fusion.40, f32[2]{0:T(128)S(1)} %get-tuple-element.28, pred[640]{0:T(1024)(128)(4,1)S(1)} %iota_compare_fusion.5), kind=kLoop, calls=%fused_computation.9 | loop fusion | flops 10240 | bytes 8328 | tf_op jit(solution)/shard_map/convert_element_type | solution.py:540
  13.3 1.9 %copy.29.s_in = bf16[512,320]{1,0:T(8,128)(2,1)} copy(bf16[512,320]{0,1:T(8,128)(2,1)} %param.15) | data formatting | bytes 655360 | tf_op args[0]
  15.2 1.9 %copy.30.t_in = bf16[512,320]{1,0:T(8,128)(2,1)} copy(bf16[512,320]{0,1:T(8,128)(2,1)} %param.16) | data formatting | bytes 655360 | tf_op args[1]
  17.1 50.0 %gather.1.w = bf16[2,16,80,640]{3,2,1,0:T(8,128)(2,1)} custom-call(bf16[32,640]{1,0:T(8,128)(2,1)} %fusion.16.pack, bf16[160,256]{1,0:T(8,128)(2,1)} %constant.84.clone.sel), custom_call_target="tpu_custom_call" | custom-call | tf_op jit(solution)/shard_map/gather/pallas_call | solution.py:166
  67.1 0.0 copy-start.6
  67.1 0.0 copy-start.9
  67.1 0.0 copy-start.1
  67.1 0.0 copy-start.5
  67.2 10.4 %step.1 = (bf16[2,16,80,384]{3,2,1,0:T(8,128)(2,1)}, f32[2,8,384]{2,1,0:T(8,128)}) custom-call(bf16[512,320]{1,0:T(8,128)(2,1)} %copy.29.s_in, bf16[512,320]{1,0:T(8,128)(2,1)} %copy.30.t_in, f32[8,384]{1,0:T(8,128)} %fusion.21.vecs, bf16[8,1280]{1,0:T(8,128)(2,1)} %pad.13.feats, f32[640,2]{1,0:T(8,128)} %fusion.7.feats_t, bf16[2,16,80,640]{3,2,1,0:T(8,128)(2,1)} %gather.1.w), custom_call_target="tpu_custom_call" | custom-call | tf_op jit(solution)/shard_map/step/pallas_call | solution.py:270
  77.5 35.5 %reduce.5 = (f32[2,16,384]{2,1,0:T(8,128)}, f32[2,8,384]{2,1,0:T(8,128)}) custom-call(bf16[2,16,80,384]{3,2,1,0:T(8,128)(2,1)} %get-tuple-element.14.grads, f32[2,8,384]{2,1,0:T(8,128)} %get-tuple-element.15.sums, bf16[2,128,80]{2,1,0:T(8,128)(2,1)} %constant.85.clone.spread), custom_call_target="tpu_custom_call" | custom-call | tf_op jit(solution)/shard_map/reduce/pallas_call | solution.py:461
  113.0 0.7 slice_reduce_fusion
  113.8 0.0 copy-start.11
  113.8 0.6 multiply_add_fusion.3
  114.4 0.6 multiply_add_fusion.4
  115.0 1.4 %multiply_add_fusion.1 = (f32[5,320]{1,0:T(8,128)}, f32[5,320]{1,0:T(8,128)}, f32[5,320]{1,0:T(8,128)}, f32[5,320]{1,0:T(8,128)}) fusion(f32[5,320]{1,0:T(8,128)S(1)} %copy-done.4, f32[5,320]{1,0:T(8,128)S(1)} %copy-done.1, f32[2,16,384]{2,1,0:T(8,128)} %get-tuple-element.16, f32[5,320]{1,0:T(8,128)S(1)} %copy-done.5, f32[5,320]{1,0:T(8,128)S(1)} %copy-done.2), kind=kLoop, calls=%fused_computation.41 | loop fusion | flops 16000 | bytes 64000 | tf_op jit(solution)/shard_map/add | solution.py:553
  116.4 1.4 %multiply_add_fusion = (f32[10,320]{1,0:T(8,128)}, f32[10,320]{1,0:T(8,128)}) fusion(f32[10,320]{1,0:T(8,128)S(1)} %copy-done.3, f32[10,320]{1,0:T(8,128)S(1)} %copy-done, f32[2,16,384]{2,1,0:T(8,128)} %get-tuple-element.16), kind=kLoop, calls=%fused_computation.25 | loop fusion | flops 16000 | bytes 64000 | tf_op jit(solution)/shard_map/add | solution.py:553
  (26 shorter events, 0.1 us)
Async XLA Ops:
  67.1 46.8 %copy-start.6 = (f32[320]{0:T(512)S(1)}, f32[320]{0:T(512)}, u32[]{:S(2)}) copy-start(f32[320]{0:T(512)} %param.27) | copy-start | bytes 3844
  67.1 46.8 %copy-start.7 = (f32[320]{0:T(512)S(1)}, f32[320]{0:T(512)}, u32[]{:S(2)}) copy-start(f32[320]{0:T(512)} %param.22) | copy-start | bytes 3844
  67.1 47.3 %copy-start.8 = (f32[320]{0:T(512)S(1)}, f32[320]{0:T(512)}, u32[]{:S(2)}) copy-start(f32[320]{0:T(512)} %param.26) | copy-start | bytes 3844
  67.1 47.3 %copy-start.9 = (f32[320]{0:T(512)S(1)}, f32[320]{0:T(512)}, u32[]{:S(2)}) copy-start(f32[320]{0:T(512)} %param.21) | copy-start | bytes 3844
  67.1 47.9 %copy-start.1 = (f32[5,320]{1,0:T(8,128)S(1)}, f32[5,320]{1,0:T(8,128)}, u32[]{:S(2)}) copy-start(f32[5,320]{1,0:T(8,128)} %param.25) | copy-start | bytes 19204
  67.1 47.9 %copy-start.2 = (f32[5,320]{1,0:T(8,128)S(1)}, f32[5,320]{1,0:T(8,128)}, u32[]{:S(2)}) copy-start(f32[5,320]{1,0:T(8,128)} %param.24) | copy-start | bytes 19204
  67.1 47.9 %copy-start.4 = (f32[5,320]{1,0:T(8,128)S(1)}, f32[5,320]{1,0:T(8,128)}, u32[]{:S(2)}) copy-start(f32[5,320]{1,0:T(8,128)} %param.20) | copy-start | bytes 19204
  67.1 47.9 %copy-start.5 = (f32[5,320]{1,0:T(8,128)S(1)}, f32[5,320]{1,0:T(8,128)}, u32[]{:S(2)}) copy-start(f32[5,320]{1,0:T(8,128)} %param.19) | copy-start | bytes 19204
  67.1 49.3 %copy-start = (f32[10,320]{1,0:T(8,128)S(1)}, f32[10,320]{1,0:T(8,128)}, u32[]{:S(2)}) copy-start(f32[10,320]{1,0:T(8,128)} %param.23) | copy-start | bytes 38404
  67.2 49.3 %copy-start.3 = (f32[10,320]{1,0:T(8,128)S(1)}, f32[10,320]{1,0:T(8,128)}, u32[]{:S(2)}) copy-start(f32[10,320]{1,0:T(8,128)} %param.18) | copy-start | bytes 38404
  113.8 4.0 %copy-start.10 = (f32[320]{0:T(512)}, f32[320]{0:T(512)S(1)}, u32[]{:S(2)}) copy-start(f32[320]{0:T(512)S(1)} %get-tuple-element.18) | copy-start | bytes 3844
  113.8 4.0 %copy-start.11 = (f32[320]{0:T(512)}, f32[320]{0:T(512)S(1)}, u32[]{:S(2)}) copy-start(f32[320]{0:T(512)S(1)} %get-tuple-element.19) | copy-start | bytes 3844
